TPU v7x, 32 devices: a whole 2x2x4 slice. The times are simulated.
32 devices in a mesh: seq: 8 (over z, x), tp: 4 (over y, core).
Axes of the slice: x: 2, y: 2, z: 4, core: 2. Of those that a mesh axis runs over, the one named last changes fastest.
Arguments:
- queries: bfloat16 [1536, 4096], P('seq', 'tp'), may hold values from -80 to 80
- keys: bfloat16 [1536, 512], P('seq', 'tp'), may hold values from -4 to 4
- values: bfloat16 [1536, 512], P('seq', 'tp'), may hold values from -6 to 6
- segment_ids: int32 [1536], P('seq'), may hold values from 0 to 15, never falling along the last dimension, each value on 1 to 1152 neighbouring positions
- out_weight: bfloat16 [4096, 8192], P('tp', 'seq'), may hold values from -0.09375 to 0.09375
Outputs:
- projected: bfloat16 [1536, 8192], P('seq', 'tp')
Inputs may be any that keep to these rules, and one draw needn't show every extreme that they name: `segment_ids`: segment numbers never fall along the sequence and every number from 0 to 15 occurs; no document has more than 1152 tokens and one has exactly that many.
All inputs are finite; a program needn't handle non-finite values.
Results may differ from a plain program's by a relative error of at most 0.012.
Values may be sent and summed in bfloat16 or wider, within the bound.
A program may use at most 128 MiB of HBM per device.

v0:
```python
import math

import jax
import jax.numpy as jnp
from jax import lax
from jax.sharding import PartitionSpec as P

HEADS = 32
KV_HEADS = 4
HEAD_DIM = 128
SEGMENTS = 16


rope_base = 500000.0
masked_score = -1e30


def rotate_heads(inputs, positions, head_dim):
    row_count = inputs.shape[0]
    head_count = inputs.shape[1] // head_dim
    half_dim = head_dim // 2
    widened = inputs.astype(jnp.float32).reshape(row_count, head_count, head_dim)
    exponent = jnp.arange(half_dim, dtype=jnp.float32) * (2.0 / head_dim)
    inverse = jnp.power(jnp.float32(rope_base), -exponent)
    angles = positions.astype(jnp.float32)[:, None] * inverse[None, :]
    cosine_table = jnp.cos(angles)[:, None, :]
    sine_table = jnp.sin(angles)[:, None, :]
    first_half = widened[:, :, :half_dim]
    second_half = widened[:, :, half_dim:]
    turned = jnp.concatenate(
        [
            first_half * cosine_table - second_half * sine_table,
            second_half * cosine_table + first_half * sine_table,
        ],
        axis=2,
    )
    return turned.reshape(row_count, head_count * head_dim).astype(jnp.bfloat16)


def doc_counts_of(segment_ids, segments):
    labels = jnp.arange(segments, dtype=jnp.int32)
    return jnp.sum((segment_ids[None, :] == labels[:, None]).astype(jnp.int32), axis=1)


def first_rows(segment, starts):
    labels = jnp.arange(starts.shape[0], dtype=jnp.int32)
    return jnp.sum(jnp.where(segment[:, None] == labels[None, :], starts[None, :], 0), axis=1)


def segment_of(global_rows, doc_ends):
    return jnp.sum((doc_ends[None, :] <= global_rows[:, None]).astype(jnp.int32), axis=1)


def block_length(piece_rows):
    for candidate in (256, 128):
        return candidate
    candidate = min(piece_rows, 256)
    while piece_rows % candidate != 0:
        candidate = candidate - 1
    return candidate


def local(queries, keys, values, segment_ids, out_weight):
    row_count = queries.shape[0]
    half_rows = row_count // 2
    my_index = lax.axis_index("seq")
    counts = doc_counts_of(segment_ids, SEGMENTS)
    totals = lax.psum(counts, "seq")
    doc_ends = jnp.cumsum(totals)
    starts = doc_ends - totals
    own_rows = my_index * row_count + jnp.arange(row_count, dtype=jnp.int32)
    positions = own_rows - first_rows(segment_ids, starts)
    query_rot = rotate_heads(queries, positions, HEAD_DIM)
    key_rot = rotate_heads(keys, positions, HEAD_DIM)
    query_segs = segment_of(own_rows, doc_ends)
    kv_local = keys.shape[1] // HEAD_DIM
    group_size = HEADS // KV_HEADS
    score_scale = 1.0 / math.sqrt(HEAD_DIM)
    query_halves = []
    for which_half in range(2):
        lower = which_half * half_rows
        query_halves.append(
            (
                query_rot[lower : lower + half_rows].reshape(
                    half_rows, kv_local, group_size, HEAD_DIM
                ),
                own_rows[lower : lower + half_rows],
                query_segs[lower : lower + half_rows],
            )
        )

    def empty_state():
        return (
            jnp.full((kv_local, group_size, half_rows), masked_score, jnp.float32),
            jnp.zeros((kv_local, group_size, half_rows), jnp.float32),
            jnp.zeros((kv_local, group_size, half_rows, HEAD_DIM), jnp.float32),
        )

    def attend_tile(carried, key_tile, value_tile, key_rows):
        key_segs = segment_of(key_rows, doc_ends)
        key_heads = key_tile.reshape(-1, kv_local, HEAD_DIM)
        value_heads = value_tile.reshape(-1, kv_local, HEAD_DIM)
        results = []
        for which_half in range(2):
            query_tile, rows_here, segs_here = query_halves[which_half]
            visible = (key_rows[None, :] <= rows_here[:, None]) & (
                key_segs[None, :] == segs_here[:, None]
            )

            def compute(running, query_tile=query_tile, visible=visible):
                row_max, normalizer, numerator = running
                scores = (
                    jnp.einsum(
                        "tkgd,skd->kgts", query_tile, key_heads, preferred_element_type=jnp.float32
                    )
                    * score_scale
                )
                scores = jnp.where(visible[None, None], scores, masked_score)
                new_max = jnp.maximum(row_max, jnp.max(scores, axis=-1))
                rescale = jnp.exp(row_max - new_max)
                weights_full = jnp.where(
                    visible[None, None], jnp.exp(scores - new_max[..., None]), 0.0
                )
                normalizer = normalizer * rescale + jnp.sum(weights_full, axis=-1)
                weights_low = weights_full.astype(jnp.bfloat16)
                numerator = numerator * rescale[..., None] + jnp.einsum(
                    "kgts,skd->kgtd", weights_low, value_heads, preferred_element_type=jnp.float32
                )
                return (new_max, normalizer, numerator)

            def keep(running):
                return running

            results.append(lax.cond(jnp.any(visible), compute, keep, carried[which_half]))
        return tuple(results)

    initial = (empty_state(), empty_state())
    key_piece = lax.all_gather(key_rot, "seq", axis=0, tiled=True)
    value_piece = lax.all_gather(values, "seq", axis=0, tiled=True)
    piece_rows = key_piece.shape[0]
    block_rows = block_length(piece_rows)

    def step(block_number, running):
        offset = block_number * block_rows
        key_tile = lax.dynamic_slice_in_dim(key_piece, offset, block_rows, 0)
        value_tile = lax.dynamic_slice_in_dim(value_piece, offset, block_rows, 0)
        key_rows = offset + jnp.arange(block_rows, dtype=jnp.int32)
        return attend_tile(running, key_tile, value_tile, key_rows)

    final = lax.fori_loop(0, piece_rows // block_rows, step, initial)
    halves_out = []
    for which_half in range(2):
        row_max, normalizer, numerator = final[which_half]
        output = numerator / normalizer[..., None]
        halves_out.append(
            jnp.transpose(output, (2, 0, 1, 3))
            .reshape(half_rows, kv_local * group_size * HEAD_DIM)
            .astype(jnp.bfloat16)
        )
    attended = jnp.concatenate(halves_out, axis=0)
    partial_value = jnp.dot(
        attended,
        lax.all_gather(out_weight, "seq", axis=1, tiled=True),
        preferred_element_type=jnp.float32,
    ).astype(jnp.bfloat16)
    summed = (
        lax.psum_scatter(partial_value, "tp", scatter_dimension=1, tiled=True)
        .astype(jnp.float32)
        .astype(jnp.bfloat16)
    )
    return summed


def solution(mesh):
    return jax.shard_map(
        local,
        mesh=mesh,
        in_specs=(P("seq", "tp"), P("seq", "tp"), P("seq", "tp"), P("seq"), P("tp", "seq")),
        out_specs=P("seq", "tp"),
        check_vma=False,
    )
```

profile of v0, /device:TPU:4, one launch (start us, length us, event | category | flops | bytes accessed | tf_op | source)
XLA Modules:
  0.0 297.8 jit_solution(15773359155438761860)
XLA Ops:
  6.5 0.7 all-gather.3.cloned.1.call-update
  7.3 0.8 convert_reduce_fusion.2
  8.1 11.6 %psum.7 = s32[16]{0:T(128)S(1)} all-reduce(s32[16]{0:T(128)S(1)} %convert_reduce_fusion.2), channel_id=1, replica_groups=mesh['seq'=8,'tp'=4] {'seq'}, use_global_device_ids=true, to_apply=%region_1.0 | all-reduce | flops 16 | bytes 128 | tf_op jit(solution)/shard_map/psum | solution.py:68
  20.0 1.1 convert_bitcast_fusion
  21.3 0.8 select_reduce_fusion
  22.1 0.4 multiply_cosine_fusion
  22.5 0.4 add_convert_fusion
  23.2 0.8 bitcast_convert_fusion
  24.1 0.5 fusion.43
  24.7 33.6 %all-gather = bf16[1536,1,128]{2,0,1:T(8,128)(2,1)S(1)} all-gather(bf16[192,1,128]{2,0,1:T(8,128)(2,1)S(1)} %pad_maximum_fusion.1), channel_id=2, replica_groups=mesh['seq'=8,'tp'=4] {'seq'}, dimensions={0}, use_global_device_ids=true | all-gather | bytes 442368 | tf_op jit(solution)/shard_map/all_gather | solution.py:138
  58.3 33.8 %all_gather.10 = bf16[1536,128]{1,0:T(8,128)(2,1)S(1)} all-gather(bf16[192,128]{1,0:T(8,128)(2,1)} %param.13), channel_id=1, replica_groups=mesh['seq'=8,'tp'=4] {'seq'}, dimensions={0}, use_global_device_ids=true | all-gather | bytes 442368 | tf_op jit(solution)/shard_map/all_gather | solution.py:139
  92.3 16.5 %while.23 = (s32[]{:T(128)}, f32[1,8,96]{2,1,0:T(8,128)S(1)}, f32[1,8,96]{2,1,0:T(8,128)S(1)}, f32[1,8,96,128]{3,2,1,0:T(8,128)S(1)}, f32[1,8,96]{2,1,0:T(8,128)...) while((s32[]{:T(128)}, f32[1,8,96]{2,1,0:T(8,128)S(1)}, ...), condition=%wide.region_17.18_spmd, body=%wide.region_5.17_spmd.sunk | while | flops 205472256 | bytes 7511063 | solution.py:150
  92.5 0.8 fusion.55
  94.6 1.2 conditional.4
  95.9 1.2 conditional.5
  95.9 0.4 fusion.50
  97.2 0.8 fusion.55
  99.6 0.8 fusion.55
  101.9 0.8 fusion.55
  104.3 0.8 fusion.55
  106.6 0.8 fusion.55
  109.4 135.7 %all-gather.3.cloned.1.call-done = bf16[1024,8192]{1,0:T(8,128)(2,1)} async-done(((bf16[1024,1024]{1,0:T(8,128)(2,1)}), bf16[1024,8192]{1,0:T(8,128)(2,1)}) %all-gather.3.cloned.1.call-update) | async-done | bytes 16777232 | tf_op jit(solution)/shard_map/all_gather | solution.py:163
  245.2 10.9 %convolution_convert_fusion = bf16[192,8192]{1,0:T(8,128)(2,1)} fusion(bf16[1024,8192]{1,0:T(8,128)(2,1)} %all-gather.3.cloned.1.call-done, bf16[96,1024]{1,0:T(8,128)(2,1)S(1)} %bitcast.119, bf16[96,1024]{1,0:T(8,128)(2,1)S(1)} %bitcast.120), kind=kOutput, calls=%fused_computation.46 | convolution fusion | flops 3223584768 | bytes 20316160 | tf_op jit(solution)/shard_map/dot_general | solution.py:161
  256.1 34.9 %reduce-scatter.2.cloned.1.call-done = bf16[192,2048]{1,0:T(8,128)(2,1)} async-done(((bf16[192,8192]{1,0:T(8,128)(2,1)}), bf16[192,2048]{1,0:T(8,128)(2,1)}) %reduce-scatter.2.cloned.1.call-update) | async-done | bytes 786448 | tf_op jit(solution)/shard_map/reduce_scatter | solution.py:167
  (68 shorter events, 4.5 us)
Async XLA Ops:
  6.5 238.6 %all-gather.3.cloned.1.call-start = ((), (), s32[]{:S(2)}) async-start(), calls=%async_computation.1 | async-start | bytes 18874368 | tf_op jit(solution)/shard_map/all_gather | solution.py:163
  7.3 283.7 %reduce-scatter.2.cloned.1.call-start = ((), (), s32[]{:S(2)}) async-start(), calls=%async_computation.2 | async-start | bytes 3932160 | tf_op jit(solution)/shard_map/reduce_scatter | solution.py:167
Sparse Core Ops, SparseCore 0:
  9.5 235.6 all-gather.2
  256.2 34.7 reduce-scatter.1
where the time goes:
time: 301 us; the launch traced here: 298 us
  waiting for transfers between devices  171 us (57%)
  blocking collectives  79 us (26%)
  between operations  13.5 us (4%)
  matrix products  12.4 us (4%)
  other arithmetic  12.1 us (4%)
  loops' own time  8.45 us (3%)
    all_gather x1, waiting for transfers between devices, local(): lax.all_gather(out_weight, 'seq', axis=1, tiled=True)  136 us
    reduce_scatter x1, waiting for transfers between devices, local(): lax.psum_scatter(partial_value, 'tp', scatter_dimension=1, tiled=True)  34.9 us
    all_gather x1, blocking collectives, local(): value_piece = lax.all_gather(values, 'seq', axis=0, tiled=True)  33.8 us
    all_gather x1, blocking collectives, local(): key_piece = lax.all_gather(key_rot, 'seq', axis=0, tiled=True)  33.6 us
    psum x1, blocking collectives, local(): totals = lax.psum(counts, 'seq')  11.6 us
    dot_general x1, matrix products, local(): jnp.dot(attended, lax.all_gather(out_weight, 'seq', axis=1, tiled=True),...  10.9 us
    another operation x1, loops' own time, local(): final = lax.fori_loop(0, piece_rows // block_rows, step, initial)  8.16 us
  transfers between devices with their start and end apart: 2, of which 2 were waited for; matrix products, arithmetic and copies ran while one was open for 5% of the time, Pallas kernels for 0%

commit v1 on v0

--- a/solution.py
+++ b/solution.py
@@ -63,16 +63,37 @@
 def local(queries, keys, values, segment_ids, out_weight):
     row_count = queries.shape[0]
     half_rows = row_count // 2
+    seq_count = lax.axis_size("seq")
+    tp_count = lax.axis_size("tp")
     my_index = lax.axis_index("seq")
-    counts = doc_counts_of(segment_ids, SEGMENTS)
-    totals = lax.psum(counts, "seq")
+    tp_index = lax.axis_index("tp")
+    pair_width = keys.shape[1] + values.shape[1]
+    id_rows = -(-row_count // pair_width)
+    pad_rows = -(-id_rows // 16) * 16
+    ids_low = jnp.pad(segment_ids.astype(jnp.bfloat16), (0, pad_rows * pair_width - row_count))
+    packed = jnp.concatenate(
+        [jnp.concatenate([keys, values], axis=1), ids_low.reshape(pad_rows, pair_width)], axis=0
+    )
+    gathered = lax.all_gather(packed, "seq", axis=0, tiled=False)
+    both = gathered[:, :row_count].reshape(seq_count * row_count, pair_width)
+    value_piece = both[:, keys.shape[1] :]
+    all_segs = (
+        gathered[:, row_count:]
+        .reshape(seq_count, pad_rows * pair_width)[:, :row_count]
+        .reshape(seq_count * row_count)
+        .astype(jnp.int32)
+    )
+    totals = doc_counts_of(all_segs, SEGMENTS)
     doc_ends = jnp.cumsum(totals)
     starts = doc_ends - totals
     own_rows = my_index * row_count + jnp.arange(row_count, dtype=jnp.int32)
     positions = own_rows - first_rows(segment_ids, starts)
     query_rot = rotate_heads(queries, positions, HEAD_DIM)
-    key_rot = rotate_heads(keys, positions, HEAD_DIM)
-    query_segs = segment_of(own_rows, doc_ends)
+    all_rows = jnp.arange(seq_count * row_count, dtype=jnp.int32)
+    key_piece = rotate_heads(
+        both[:, : keys.shape[1]], all_rows - first_rows(all_segs, starts), HEAD_DIM
+    )
+    query_segs = segment_ids
     kv_local = keys.shape[1] // HEAD_DIM
     group_size = HEADS // KV_HEADS
     score_scale = 1.0 / math.sqrt(HEAD_DIM)
@@ -135,8 +156,6 @@
         return tuple(results)
 
     initial = (empty_state(), empty_state())
-    key_piece = lax.all_gather(key_rot, "seq", axis=0, tiled=True)
-    value_piece = lax.all_gather(values, "seq", axis=0, tiled=True)
     piece_rows = key_piece.shape[0]
     block_rows = block_length(piece_rows)
 
@@ -158,17 +177,36 @@
             .astype(jnp.bfloat16)
         )
     attended = jnp.concatenate(halves_out, axis=0)
+    attended_all = lax.all_gather(attended, "seq", axis=0, tiled=True)
     partial_value = jnp.dot(
-        attended,
-        lax.all_gather(out_weight, "seq", axis=1, tiled=True),
-        preferred_element_type=jnp.float32,
+        attended_all, out_weight, preferred_element_type=jnp.float32
     ).astype(jnp.bfloat16)
-    summed = (
-        lax.psum_scatter(partial_value, "tp", scatter_dimension=1, tiled=True)
-        .astype(jnp.float32)
-        .astype(jnp.bfloat16)
-    )
-    return summed
+    return spread(partial_value, row_count)
+
+
+def spread(partial_value, row_count):
+    seq_count = lax.axis_size("seq")
+    tp_count = lax.axis_size("tp")
+    per = seq_count // tp_count
+    my_index = lax.axis_index("seq")
+    summed = lax.psum_scatter(partial_value, "tp", scatter_dimension=0, tiled=True)
+    width = summed.shape[1]
+    blocks = summed.reshape(per, row_count, width)
+    arrived = []
+    for slot in range(per):
+        pairs = []
+        for j in range(seq_count):
+            for k in range(tp_count):
+                i = k * per + (slot + j) % per
+                pairs.append((j * tp_count + k, i * tp_count + j // per))
+        outgoing = lax.dynamic_index_in_dim(blocks, (slot + my_index) % per, 0, keepdims=False)
+        arrived.append(lax.ppermute(outgoing, ("seq", "tp"), pairs))
+    stacked = jnp.stack(arrived, axis=0)
+    order = (my_index - jnp.arange(per, dtype=jnp.int32)) % per
+    return jnp.concatenate(
+        [lax.dynamic_index_in_dim(stacked, order[c], 0, keepdims=False) for c in range(per)],
+        axis=1,
+    )
 
 
 def solution(mesh):

time: 301 us -> 242 us (0.80); the launches traced: 298 us -> 242 us
  blocking collectives: 79 us -> 32.5 us
  waiting for transfers between devices: 171 us -> 137 us
  local copies, waits for them, and re-layouts: 0.83 us -> 16.2 us
  starting transfers between devices: 0.04 us -> 6.95 us
  matrix products: 12.4 us -> 8.36 us
  other arithmetic: 12.1 us -> 16.1 us
  between operations: 13.5 us -> 17.5 us
    all_gather x1, waiting for transfers between devices: 136 us -> 70.7 us  [local(): attended_all = lax.all_gather(attended, 'seq', axis=0, tiled=True)]
    all_gather x2 -> x1, blocking collectives: 67.4 us -> 32.5 us  [local(): gathered = lax.all_gather(packed, 'seq', axis=0, tiled=False)]
    ppermute x0 -> x2, waiting for transfers between devices: none -> 30.2 us  [spread(): arrived.append(lax.ppermute(outgoing, ('seq', 'tp'), pairs))]
    psum x1 -> x0, blocking collectives: 11.6 us -> none  [local(): totals = lax.psum(counts, 'seq')]
    ppermute x0 -> x2, starting transfers between devices: none -> 6.91 us  [spread(): arrived.append(lax.ppermute(outgoing, ('seq', 'tp'), pairs))]
    dynamic_slice x0 -> x12, local copies, waits for them, and re-layouts: none -> 5.73 us  [step(): key_tile = lax.dynamic_slice_in_dim(key_piece, offset, block_rows, 0)]
    reshape x6, local copies, waits for them, and re-layouts: 0.11 us -> 5.11 us  [attend_tile(): value_heads = value_tile.reshape(-1, kv_local, HEAD_DIM)]
    dot_general x1, matrix products: 10.9 us -> 6.78 us  [local(): jnp.dot(attended_all, out_weight, preferred_element_type=jnp.float32)]
  transfers between devices with their start and end apart: 2 -> 4, of which waited for: 2 -> 4; matrix products, arithmetic and copies ran while one was open for 5% -> 0% of each run, Pallas kernels for 0% -> 0%
where the time goes in v1:
time: 242 us
  waiting for transfers between devices  137 us (57%)
  blocking collectives  32.5 us (13%)
  between operations  17.5 us (7%)
  local copies, waits for them, and re-layouts  16.2 us (7%)
  other arithmetic  16.1 us (7%)
  matrix products  8.36 us (3%)
  loops' own time  8.04 us (3%)
  starting transfers between devices  6.95 us (3%)
    all_gather x1, waiting for transfers between devices, local(): attended_all = lax.all_gather(attended, 'seq', axis=0, tiled=True)  70.7 us
    reduce_scatter x1, waiting for transfers between devices, spread(): lax.psum_scatter(partial_value, 'tp', scatter_dimension=0, tiled=True)  35.6 us
    all_gather x1, blocking collectives, local(): gathered = lax.all_gather(packed, 'seq', axis=0, tiled=False)  32.5 us
    ppermute x2, waiting for transfers between devices, spread(): arrived.append(lax.ppermute(outgoing, ('seq', 'tp'), pairs))  30.2 us
    another operation x1, loops' own time, local(): final = lax.fori_loop(0, piece_rows // block_rows, step, initial)  7.82 us
    ppermute x2, starting transfers between devices, spread(): arrived.append(lax.ppermute(outgoing, ('seq', 'tp'), pairs))  6.91 us
    dot_general x1, matrix products, local(): jnp.dot(attended_all, out_weight, preferred_element_type=jnp.float32)  6.78 us
    dynamic_slice x12, local copies, waits for them, and re-layouts, step(): key_tile = lax.dynamic_slice_in_dim(key_piece, offset, block_rows, 0)  5.73 us
  transfers between devices with their start and end apart: 4, of which 4 were waited for; matrix products, arithmetic and copies ran while one was open for 0% of the time, Pallas kernels for 0%

profile of v1, /device:TPU:4, one launch (start us, length us, event | category | flops | bytes accessed | tf_op | source)
XLA Modules:
  0.0 242.1 jit_solution(10967941362189829822)
XLA Ops:
  6.6 0.9 convert_element_type.92
  8.3 32.5 %all-gather = bf16[1664,256]{1,0:T(8,128)(2,1)S(1)} all-gather(bf16[208,256]{1,0:T(8,128)(2,1)S(1)} %pad_maximum_fusion.3), channel_id=2, replica_groups=mesh['seq'=8,'tp'=4] {'seq'}, dimensions={0}, use_global_device_ids=true | all-gather | bytes 958464 | tf_op jit(solution)/shard_map/all_gather | solution.py:77
  42.1 0.9 slice.72
  46.5 1.6 fusion.35
  49.0 26.7 %while.23 = (s32[]{:T(128)}, f32[1,8,96]{2,1,0:T(8,128)S(1)}, f32[1,8,96]{2,1,0:T(8,128)S(1)}, f32[1,8,96,128]{3,2,1,0:T(8,128)S(1)}, f32[1,8,96]{2,1,0:T(8,128)...) while((s32[]{:T(128)}, f32[1,8,96]{2,1,0:T(8,128)S(1)}, ...), condition=%wide.region_16.17_spmd, body=%wide.region_4.16_spmd.sunk | while | flops 205472256 | bytes 7642139 | solution.py:169
  50.9 0.9 dynamic-slice_bitcast_fusion.4
  52.4 1.2 conditional.5
  54.2 1.2 conditional.4
  57.4 0.9 dynamic-slice_bitcast_fusion.4
  61.4 0.9 dynamic-slice_bitcast_fusion.4
  65.4 0.9 dynamic-slice_bitcast_fusion.4
  68.5 0.8 constant_dynamic-slice_fusion.2
  69.5 0.9 dynamic-slice_bitcast_fusion.4
  73.5 0.9 dynamic-slice_bitcast_fusion.4
  77.2 70.7 %all-gather.3.cloned.1.call-done = bf16[1536,1024]{1,0:T(8,128)(2,1)} async-done(((bf16[192,1024]{1,0:T(8,128)(2,1)}), bf16[1536,1024]{1,0:T(8,128)(2,1)}) %all-gather.3.cloned.1.call-update) | async-done | bytes 3145744 | tf_op jit(solution)/shard_map/all_gather | solution.py:180
  147.9 6.8 %convolution_convert_fusion = bf16[1536,1024]{1,0:T(8,128)(2,1)} fusion(bf16[1536,1024]{1,0:T(8,128)(2,1)} %all-gather.3.cloned.1.call-done, bf16[1024,1024]{1,0:T(8,128)(2,1)S(1)} %copy-done), kind=kOutput, calls=%fused_computation.46 | convolution fusion | flops 3222798336 | bytes 8388608 | tf_op jit(solution)/shard_map/dot_general | solution.py:181
  154.7 35.6 %reduce-scatter.2.cloned.1.call-done = bf16[384,1024]{1,0:T(8,128)(2,1)} async-done(((bf16[1536,1024]{1,0:T(8,128)(2,1)}), bf16[384,1024]{1,0:T(8,128)(2,1)}) %reduce-scatter.2.cloned.1.call-update) | async-done | bytes 786448 | tf_op jit(solution)/shard_map/reduce_scatter | solution.py:192
  190.2 1.2 dynamic-slice_bitcast_fusion.1
  191.4 5.4 %collective-permute-start = (bf16[192,1024]{1,0:T(8,128)(2,1)S(1)}, bf16[192,1024]{1,0:T(8,128)(2,1)S(1)}, u32[]{:S(2)}, u32[]{:S(2)}) collective-permute-start(bf16[192,1024]{1,0:T(8,128)(2,1)S(1)} %get-tuple-element.460), channel_id=1, source_target_pairs={{0,0},{1,8},{2,16},{3,24},{4,4},{5,12},{6,20},{7,28},{8,1},{9,9},{... | collective-permute-start | bytes 1179656 | tf_op jit(solution)/shard_map/ppermute | solution.py:203
  196.8 1.5 collective-permute-start.1
  202.8 21.1 %collective-permute-done = bf16[192,1024]{1,0:T(8,128)(2,1)S(1)} collective-permute-done((bf16[192,1024]{1,0:T(8,128)(2,1)S(1)}, bf16[192,1024]{1,0:T(8,128)(2,1)S(1)}, u32[]{:S(2)}, u32[]{:S(2)}) %collective-permute-start) | collective-permute-done | bytes 393248 | tf_op jit(solution)/shard_map/ppermute | solution.py:203
  223.8 9.2 %collective-permute-done.1 = bf16[192,1024]{1,0:T(8,128)(2,1)} collective-permute-done((bf16[192,1024]{1,0:T(8,128)(2,1)S(1)}, bf16[192,1024]{1,0:T(8,128)(2,1)}, u32[]{:S(2)}, u32[]{:S(2)}) %collective-permute-start.1) | collective-permute-done | bytes 393248 | tf_op jit(solution)/shard_map/ppermute | solution.py:203
  233.0 1.3 fusion.41
  234.3 0.9 pad_maximum_fusion
  (106 shorter events, 21.3 us)
Async XLA Ops:
  6.5 141.3 %copy-start = (bf16[1024,1024]{1,0:T(8,128)(2,1)S(1)}, bf16[1024,1024]{1,0:T(8,128)(2,1)}, u32[]{:S(2)}) copy-start(bf16[1024,1024]{1,0:T(8,128)(2,1)} %param.15) | copy-start | bytes 6291460
  6.5 37.3 %copy-start.2 = (bf16[192,1024]{1,0:T(8,128)(2,1)S(1)}, bf16[192,1024]{1,0:T(8,128)(2,1)}, u32[]{:S(2)}) copy-start(bf16[192,1024]{1,0:T(8,128)(2,1)} %param.11) | copy-start | bytes 1179652
  6.5 141.3 %all-gather.3.cloned.1.call-start = ((), (), s32[]{:S(2)}) async-start(), calls=%async_computation.1 | async-start | bytes 3538944 | tf_op jit(solution)/shard_map/all_gather | solution.py:180
  44.1 1.2 copy-start.1
  77.1 113.1 %reduce-scatter.2.cloned.1.call-start = ((), (), s32[]{:S(2)}) async-start(), calls=%async_computation.2 | async-start | bytes 3932160 | tf_op jit(solution)/shard_map/reduce_scatter | solution.py:192
  191.4 32.4 %collective-permute-start = (bf16[192,1024]{1,0:T(8,128)(2,1)S(1)}, bf16[192,1024]{1,0:T(8,128)(2,1)S(1)}, u32[]{:S(2)}, u32[]{:S(2)}) collective-permute-start(bf16[192,1024]{1,0:T(8,128)(2,1)S(1)} %get-tuple-element.460), channel_id=1, source_target_pairs={{0,0},{1,8},{2,16},{3,24},{4,4},{5,12},{6,20},{7,28},{8,1},{9,9},{... | collective-permute-start | bytes 1179656 | tf_op jit(solution)/shard_map/ppermute | solution.py:203
  196.8 36.2 %collective-permute-start.1 = (bf16[192,1024]{1,0:T(8,128)(2,1)S(1)}, bf16[192,1024]{1,0:T(8,128)(2,1)}, u32[]{:S(2)}, u32[]{:S(2)}) collective-permute-start(bf16[192,1024]{1,0:T(8,128)(2,1)S(1)} %get-tuple-element.459), channel_id=1, source_target_pairs={{0,4},{1,12},{2,20},{3,28},{4,0},{5,8},{6,16},{7,24},{8,5},{9,13},... | collective-permute-start | bytes 1179656 | tf_op jit(solution)/shard_map/ppermute | solution.py:203
Sparse Core Ops, SparseCore 0:
  77.2 70.5 all-gather.2
  154.8 35.4 reduce-scatter.1

commit v2 on v1

--- a/solution.py
+++ b/solution.py
@@ -1,8 +1,11 @@
+import functools
 import math
 
 import jax
 import jax.numpy as jnp
 from jax import lax
+from jax.experimental import pallas as pl
+from jax.experimental.pallas import tpu as pltpu
 from jax.sharding import PartitionSpec as P
 
 HEADS = 32
@@ -60,13 +63,59 @@
     return candidate
 
 
+def gather_kernel(members, stride, own_ref, all_ref, send_sems, recv_sems):
+    me = lax.axis_index("seq")
+    slot = lax.div(me, stride)
+    place = lax.rem(me, stride)
+    peers = [lax.rem(slot + d, members) * stride + place for d in range(1, members)]
+    barrier = pltpu.get_barrier_semaphore()
+    for peer in peers:
+        pl.semaphore_signal(
+            barrier, inc=1, device_id={"seq": peer}, device_id_type=pl.DeviceIdType.MESH
+        )
+    pl.semaphore_wait(barrier, members - 1)
+    copies = []
+    for d, peer in enumerate(peers):
+        copy = pltpu.make_async_remote_copy(
+            src_ref=own_ref,
+            dst_ref=all_ref.at[slot],
+            send_sem=send_sems.at[d],
+            recv_sem=recv_sems.at[d],
+            device_id={"seq": peer},
+            device_id_type=pl.DeviceIdType.MESH,
+        )
+        copy.start()
+        copies.append(copy)
+    all_ref[slot] = own_ref[...]
+    for copy in copies:
+        copy.wait()
+
+
+def direct_gather(own, members, stride, collective_id):
+    moved = own.size * own.dtype.itemsize * (members - 1)
+    return pl.pallas_call(
+        functools.partial(gather_kernel, members, stride),
+        out_shape=jax.ShapeDtypeStruct((members,) + own.shape, own.dtype),
+        in_specs=[pl.BlockSpec(memory_space=pltpu.VMEM)],
+        out_specs=pl.BlockSpec(memory_space=pltpu.VMEM),
+        scratch_shapes=[
+            pltpu.SemaphoreType.DMA((members - 1,)),
+            pltpu.SemaphoreType.DMA((members - 1,)),
+        ],
+        compiler_params=pltpu.CompilerParams(
+            collective_id=collective_id, has_side_effects=True
+        ),
+        cost_estimate=pl.CostEstimate(flops=0, bytes_accessed=20 * moved, transcendentals=0),
+    )(own)
+
+
 def local(queries, keys, values, segment_ids, out_weight):
     row_count = queries.shape[0]
     half_rows = row_count // 2
     seq_count = lax.axis_size("seq")
     tp_count = lax.axis_size("tp")
     my_index = lax.axis_index("seq")
-    tp_index = lax.axis_index("tp")
+    per = seq_count // tp_count
     pair_width = keys.shape[1] + values.shape[1]
     id_rows = -(-row_count // pair_width)
     pad_rows = -(-id_rows // 16) * 16
@@ -74,7 +123,16 @@
     packed = jnp.concatenate(
         [jnp.concatenate([keys, values], axis=1), ids_low.reshape(pad_rows, pair_width)], axis=0
     )
-    gathered = lax.all_gather(packed, "seq", axis=0, tiled=False)
+    weight_wide = lax.all_gather(
+        out_weight,
+        "seq",
+        axis=1,
+        tiled=True,
+        axis_index_groups=[
+            [t * per + r for r in range(per)] for t in range(tp_count)
+        ],
+    )
+    gathered = direct_gather(packed, seq_count, 1, 0)
     both = gathered[:, :row_count].reshape(seq_count * row_count, pair_width)
     value_piece = both[:, keys.shape[1] :]
     all_segs = (
@@ -177,36 +235,19 @@
             .astype(jnp.bfloat16)
         )
     attended = jnp.concatenate(halves_out, axis=0)
-    attended_all = lax.all_gather(attended, "seq", axis=0, tiled=True)
+    attended_all = direct_gather(attended, tp_count, per, 1).reshape(
+        tp_count * row_count, attended.shape[1]
+    )
     partial_value = jnp.dot(
-        attended_all, out_weight, preferred_element_type=jnp.float32
+        attended_all, weight_wide, preferred_element_type=jnp.float32
     ).astype(jnp.bfloat16)
-    return spread(partial_value, row_count)
-
-
-def spread(partial_value, row_count):
-    seq_count = lax.axis_size("seq")
-    tp_count = lax.axis_size("tp")
-    per = seq_count // tp_count
-    my_index = lax.axis_index("seq")
     summed = lax.psum_scatter(partial_value, "tp", scatter_dimension=0, tiled=True)
-    width = summed.shape[1]
-    blocks = summed.reshape(per, row_count, width)
-    arrived = []
-    for slot in range(per):
-        pairs = []
-        for j in range(seq_count):
+    pairs = []
+    for t in range(tp_count):
+        for r in range(per):
             for k in range(tp_count):
-                i = k * per + (slot + j) % per
-                pairs.append((j * tp_count + k, i * tp_count + j // per))
-        outgoing = lax.dynamic_index_in_dim(blocks, (slot + my_index) % per, 0, keepdims=False)
-        arrived.append(lax.ppermute(outgoing, ("seq", "tp"), pairs))
-    stacked = jnp.stack(arrived, axis=0)
-    order = (my_index - jnp.arange(per, dtype=jnp.int32)) % per
-    return jnp.concatenate(
-        [lax.dynamic_index_in_dim(stacked, order[c], 0, keepdims=False) for c in range(per)],
-        axis=1,
-    )
+                pairs.append(((t * per + r) * tp_count + k, (k * per + r) * tp_count + t))
+    return lax.ppermute(summed, ("seq", "tp"), pairs)
 
 
 def solution(mesh):

time: 242 us -> 201 us (0.83)
  Pallas kernels: 0 us -> 64.3 us
  waiting for transfers between devices: 137 us -> 80.6 us
  blocking collectives: 32.5 us -> 0 us
  local copies, waits for them, and re-layouts: 16.2 us -> 5.58 us
  between operations: 17.5 us -> 13.7 us
  other arithmetic: 16.1 us -> 13 us
    all_gather x1, waiting for transfers between devices: 70.7 us -> 0.02 us  [local(): lax.all_gather(out_weight, 'seq', axis=1, tiled=True, axis_index_groups=[...]
    pallas_call x0 -> x2, Pallas kernels: none -> 64.3 us  [direct_gather(): pl.pallas_call(functools.partial(gather_kernel, members, stride), out_sha...]
    all_gather x1 -> x0, blocking collectives: 32.5 us -> none  [local(): gathered = lax.all_gather(packed, 'seq', axis=0, tiled=False)]
    reduce_scatter x1, waiting for transfers between devices: 35.6 us -> 44.5 us  [local(): lax.psum_scatter(partial_value, 'tp', scatter_dimension=0, tiled=True)]
    ppermute x2 -> x1, waiting for transfers between devices: 30.2 us -> 35.4 us  [local(): return lax.ppermute(summed, ('seq', 'tp'), pairs)]
    reshape x6, local copies, waits for them, and re-layouts: 5.11 us -> 0.09 us  [attend_tile(): value_heads = value_tile.reshape(-1, kv_local, HEAD_DIM)]
    dynamic_slice x12, local copies, waits for them, and re-layouts: 5.73 us -> 0.75 us  [step(): key_tile = lax.dynamic_slice_in_dim(key_piece, offset, block_rows, 0)]
    ppermute x2 -> x1, starting transfers between devices: 6.91 us -> 5.44 us  [local(): return lax.ppermute(summed, ('seq', 'tp'), pairs)]
  transfers between devices with their start and end apart: 4 -> 3, of which waited for: 4 -> 2; matrix products, arithmetic and copies ran while one was open for 0% -> 10% of each run, Pallas kernels for 0% -> 32%
where the time goes in v2:
time: 201 us
  waiting for transfers between devices  80.6 us (40%)
  Pallas kernels  64.3 us (32%)
  between operations  13.7 us (7%)
  other arithmetic  13 us (6%)
  matrix products  9.34 us (5%)
  loops' own time  8.53 us (4%)
  local copies, waits for them, and re-layouts  5.58 us (3%)
  starting transfers between devices  5.48 us (3%)
    pallas_call x2, Pallas kernels, direct_gather(): pl.pallas_call(functools.partial(gather_kernel, members, stride), out_sha...  64.3 us
    reduce_scatter x1, waiting for transfers between devices, local(): lax.psum_scatter(partial_value, 'tp', scatter_dimension=0, tiled=True)  44.5 us
    ppermute x1, waiting for transfers between devices, local(): return lax.ppermute(summed, ('seq', 'tp'), pairs)  35.4 us
    another operation x1, loops' own time, local(): final = lax.fori_loop(0, piece_rows // block_rows, step, initial)  8.24 us
    dot_general x1, matrix products, local(): jnp.dot(attended_all, weight_wide, preferred_element_type=jnp.float32)  7.76 us
    ppermute x1, starting transfers between devices, local(): return lax.ppermute(summed, ('seq', 'tp'), pairs)  5.44 us
    reduce_or x6, other arithmetic, attend_tile(): jnp.any(visible)  4.99 us
  transfers between devices with their start and end apart: 3, of which 2 were waited for; matrix products, arithmetic and copies ran while one was open for 10% of the time, Pallas kernels for 32%

profile of v2, /device:TPU:4, one launch (start us, length us, event | category | flops | bytes accessed | tf_op | source)
XLA Modules:
  0.0 200.6 jit_solution(2052698145753369490)
XLA Ops:
  6.5 0.7 all-gather.2.cloned.1.call-update
  7.3 0.7 convert_element_type.92
  8.0 0.8 fusion.48
  8.9 1.5 pad_maximum_fusion.2.own_ref
  10.3 20.2 %shard_map.55 = bf16[8,208,256]{2,1,0:T(8,128)(2,1)} custom-call(bf16[208,256]{1,0:T(8,128)(2,1)} %pad_maximum_fusion.2.own_ref), custom_call_target="tpu_custom_call" | custom-call | bytes 14909440 | tf_op jit(solution)/shard_map/pallas_call | solution.py:96
  30.5 0.9 slice_bitcast_fusion
  31.4 1.2 slice.51
  35.1 1.6 fusion.35
  36.9 17.3 %while.23 = (s32[]{:T(128)}, f32[1,8,96]{2,1,0:T(8,128)S(1)}, f32[1,8,96]{2,1,0:T(8,128)S(1)}, f32[1,8,96,128]{3,2,1,0:T(8,128)S(1)}, f32[1,8,96]{2,1,0:T(8,128)...) while((s32[]{:T(128)}, f32[1,8,96]{2,1,0:T(8,128)S(1)}, ...), condition=%wide.region_16.17_spmd, body=%wide.region_4.16_spmd.sunk | while | flops 205472256 | bytes 7642139 | solution.py:227
  37.0 0.8 fusion.53
  39.3 1.2 conditional.4
  40.6 1.2 conditional.5
  41.9 0.8 fusion.53
  44.4 0.8 fusion.53
  46.9 0.8 fusion.53
  49.4 0.8 fusion.53
  51.8 0.8 fusion.53
  54.8 0.8 pad_maximum_fusion.own_ref
  55.6 44.1 %shard_map.56 = bf16[4,192,1024]{2,1,0:T(8,128)(2,1)} custom-call(bf16[192,1024]{1,0:T(8,128)(2,1)} %pad_maximum_fusion.own_ref), custom_call_target="tpu_custom_call" | custom-call | bytes 23592960 | tf_op jit(solution)/shard_map/pallas_call | solution.py:96
  99.7 7.8 %convolution_convert_fusion = bf16[768,2048]{1,0:T(8,128)(2,1)} fusion(bf16[768,1024]{1,0:T(8,128)(2,1)} %bitcast.125, bf16[1024,2048]{1,0:T(8,128)(2,1)} %all-gather.2.cloned.1.call-done), kind=kOutput, calls=%fused_computation.46 | convolution fusion | flops 3222798336 | bytes 8912896 | tf_op jit(solution)/shard_map/dot_general | solution.py:241
  107.5 44.5 %reduce-scatter.2.cloned.1.call-done = bf16[192,2048]{1,0:T(8,128)(2,1)} async-done(((bf16[768,2048]{1,0:T(8,128)(2,1)}), bf16[192,2048]{1,0:T(8,128)(2,1)}) %reduce-scatter.2.cloned.1.call-update) | async-done | bytes 786448 | tf_op jit(solution)/shard_map/reduce_scatter | solution.py:244
  152.0 5.4 %collective-permute-start = (bf16[192,2048]{1,0:T(8,128)(2,1)}, bf16[192,2048]{1,0:T(8,128)(2,1)S(1)}, u32[]{:S(2)}, u32[]{:S(2)}) collective-permute-start(bf16[192,2048]{1,0:T(8,128)(2,1)} %reduce-scatter.2.cloned.1.call-done), channel_id=1, source_target_pairs={{0,0},{1,8},{2,16},{3,24},{4,4},{5,12},{6,20},{7,28},{8,1},{9,9},{... | collective-permute-start | bytes 2359304 | tf_op jit(solution)/shard_map/ppermute | solution.py:250
  157.5 35.4 %collective-permute-done = bf16[192,2048]{1,0:T(8,128)(2,1)S(1)} collective-permute-done((bf16[192,2048]{1,0:T(8,128)(2,1)}, bf16[192,2048]{1,0:T(8,128)(2,1)S(1)}, u32[]{:S(2)}, u32[]{:S(2)}) %collective-permute-start) | collective-permute-done | bytes 786464 | tf_op jit(solution)/shard_map/ppermute | solution.py:250
  192.8 0.9 copy.72
  (99 shorter events, 7.1 us)
Async XLA Ops:
  6.5 26.6 %copy-start.1 = (s32[192]{0:T(256)S(1)}, s32[192]{0:T(256)}, u32[]{:S(2)}) copy-start(s32[192]{0:T(256)} %param.14) | copy-start | bytes 2308
  6.5 93.2 %all-gather.2.cloned.1.call-start = ((), (), s32[]{:S(2)}) async-start(), calls=%async_computation.1 | async-start | bytes 6291456 | tf_op jit(solution)/shard_map/all_gather | solution.py:126
  7.3 144.8 %reduce-scatter.2.cloned.1.call-start = ((), (), s32[]{:S(2)}) async-start(), calls=%async_computation.2 | async-start | bytes 3932160 | tf_op jit(solution)/shard_map/reduce_scatter | solution.py:244
  10.3 23.4 %copy-start = (bf16[192,1024]{1,0:T(8,128)(2,1)S(1)}, bf16[192,1024]{1,0:T(8,128)(2,1)}, u32[]{:S(2)}) copy-start(bf16[192,1024]{1,0:T(8,128)(2,1)} %param.11) | copy-start | bytes 1179652
  152.0 40.8 %collective-permute-start = (bf16[192,2048]{1,0:T(8,128)(2,1)}, bf16[192,2048]{1,0:T(8,128)(2,1)S(1)}, u32[]{:S(2)}, u32[]{:S(2)}) collective-permute-start(bf16[192,2048]{1,0:T(8,128)(2,1)} %reduce-scatter.2.cloned.1.call-done), channel_id=1, source_target_pairs={{0,0},{1,8},{2,16},{3,24},{4,4},{5,12},{6,20},{7,28},{8,1},{9,9},{... | collective-permute-start | bytes 2359304 | tf_op jit(solution)/shard_map/ppermute | solution.py:250
Sparse Core Ops, SparseCore 0:
  8.9 62.1 all-gather.1
  107.6 44.3 reduce-scatter.1

commit v3 on v2

v3 whole, which is shorter than its diff:
```python
import functools
import math

import jax
import jax.numpy as jnp
from jax import lax
from jax.experimental import pallas as pl
from jax.experimental.pallas import tpu as pltpu
from jax.sharding import PartitionSpec as P

HEADS = 32
KV_HEADS = 4
HEAD_DIM = 128
SEGMENTS = 16


rope_base = 500000.0
masked_score = -1e30


def rotate_heads(inputs, positions, head_dim):
    row_count = inputs.shape[0]
    head_count = inputs.shape[1] // head_dim
    half_dim = head_dim // 2
    widened = inputs.astype(jnp.float32).reshape(row_count, head_count, head_dim)
    exponent = jnp.arange(half_dim, dtype=jnp.float32) * (2.0 / head_dim)
    inverse = jnp.power(jnp.float32(rope_base), -exponent)
    angles = positions.astype(jnp.float32)[:, None] * inverse[None, :]
    cosine_table = jnp.cos(angles)[:, None, :]
    sine_table = jnp.sin(angles)[:, None, :]
    first_half = widened[:, :, :half_dim]
    second_half = widened[:, :, half_dim:]
    turned = jnp.concatenate(
        [
            first_half * cosine_table - second_half * sine_table,
            second_half * cosine_table + first_half * sine_table,
        ],
        axis=2,
    )
    return turned.reshape(row_count, head_count * head_dim).astype(jnp.bfloat16)


def doc_counts_of(segment_ids, segments):
    labels = jnp.arange(segments, dtype=jnp.int32)
    return jnp.sum((segment_ids[None, :] == labels[:, None]).astype(jnp.int32), axis=1)


def first_rows(segment, starts):
    labels = jnp.arange(starts.shape[0], dtype=jnp.int32)
    return jnp.sum(jnp.where(segment[:, None] == labels[None, :], starts[None, :], 0), axis=1)


def attend_kernel(
    group_size, limits, query_ref, key_ref, value_ref, qseg_ref, kseg_ref, out_ref, top, total, acc
):
    row_count = query_ref.shape[0]
    block_rows = kseg_ref.shape[2]
    head_count = query_ref.shape[1] // HEAD_DIM
    score_scale = 1.0 / math.sqrt(HEAD_DIM)
    top[...] = jnp.full(top.shape, 0.5 * masked_score, jnp.float32)
    total[...] = jnp.zeros(total.shape, jnp.float32)
    acc[...] = jnp.zeros(acc.shape, jnp.float32)

    def tile(number, unused):
        offset = pl.multiple_of(number * block_rows, block_rows)
        key_rows = offset + lax.broadcasted_iota(jnp.int32, (row_count, block_rows), 1)
        rows = limits[2] + lax.broadcasted_iota(jnp.int32, (row_count, block_rows), 0)
        visible = (key_rows <= rows) & (kseg_ref[number] == qseg_ref[...])
        for head in range(head_count):
            lanes = slice(head * HEAD_DIM, (head + 1) * HEAD_DIM)
            kv = head // group_size
            kv_lanes = slice(kv * HEAD_DIM, (kv + 1) * HEAD_DIM)
            scores = lax.dot_general(
                query_ref[:, lanes],
                key_ref[pl.ds(offset, block_rows), kv_lanes],
                (((1,), (1,)), ((), ())),
                preferred_element_type=jnp.float32,
            )
            scores = jnp.where(visible, scores * score_scale, masked_score)
            old = top[head]
            new = jnp.maximum(old, jnp.max(scores, axis=1, keepdims=True))
            rescale = jnp.exp(old - new)
            weights = jnp.exp(scores - new)
            top[head] = new
            total[head] = total[head] * rescale + jnp.sum(weights, axis=1, keepdims=True)
            acc[head] = acc[head] * rescale + jnp.dot(
                weights.astype(jnp.bfloat16),
                value_ref[pl.ds(offset, block_rows), kv_lanes],
                preferred_element_type=jnp.float32,
            )
        return unused

    lax.fori_loop(limits[0], limits[1], tile, 0)
    for head in range(head_count):
        out_ref[:, head * HEAD_DIM : (head + 1) * HEAD_DIM] = (acc[head] / total[head]).astype(
            out_ref.dtype
        )


def attend(query_rot, key_piece, value_piece, query_segs, key_segs, first_row, first_position):
    row_count = query_rot.shape[0]
    token_count = key_piece.shape[0]
    block_rows = 256 if token_count % 256 == 0 else row_count
    head_count = query_rot.shape[1] // HEAD_DIM
    limits = jnp.stack(
        [
            (first_row - first_position) // block_rows,
            (first_row + row_count - 1) // block_rows + 1,
            first_row,
        ]
    ).astype(jnp.int32)
    vmem = pl.BlockSpec(memory_space=pltpu.VMEM)
    return pl.pallas_call(
        functools.partial(attend_kernel, HEADS // KV_HEADS),
        out_shape=jax.ShapeDtypeStruct(query_rot.shape, query_rot.dtype),
        in_specs=[pl.BlockSpec(memory_space=pltpu.SMEM)] + [vmem] * 5,
        out_specs=vmem,
        scratch_shapes=[
            pltpu.VMEM((head_count, row_count, 1), jnp.float32),
            pltpu.VMEM((head_count, row_count, 1), jnp.float32),
            pltpu.VMEM((head_count, row_count, HEAD_DIM), jnp.float32),
        ],
        cost_estimate=pl.CostEstimate(
            flops=4 * row_count * token_count * query_rot.shape[1],
            bytes_accessed=2 * (query_rot.size * 2 + key_piece.size * 2),
            transcendentals=row_count * token_count * head_count,
        ),
    )(
        limits,
        query_rot,
        key_piece,
        value_piece,
        query_segs[:, None],
        key_segs.reshape(token_count // block_rows, 1, block_rows),
    )


def gather_kernel(members, stride, spread_out, own_ref, all_ref, send_sems, recv_sems):
    me = lax.axis_index("seq")
    slot = lax.div(me, stride)
    place = lax.rem(me, stride)
    peers = [lax.rem(slot + d, members) * stride + place for d in range(1, members)]
    barrier = pltpu.get_barrier_semaphore()
    for peer in peers:
        pl.semaphore_signal(
            barrier, inc=1, device_id={"seq": peer}, device_id_type=pl.DeviceIdType.MESH
        )
    pl.semaphore_wait(barrier, members - 1)
    keep = slot if spread_out is None else spread_out(slot)
    copies = []
    for d, peer in enumerate(peers):
        copy = pltpu.make_async_remote_copy(
            src_ref=own_ref,
            dst_ref=all_ref.at[keep],
            send_sem=send_sems.at[d],
            recv_sem=recv_sems.at[d],
            device_id={"seq": peer},
            device_id_type=pl.DeviceIdType.MESH,
        )
        copy.start()
        copies.append(copy)
    all_ref[keep] = own_ref[...]
    for copy in copies:
        copy.wait()


def direct_gather(own, members, stride, collective_id, spread_out=None):
    moved = own.size * own.dtype.itemsize * (members - 1)
    return pl.pallas_call(
        functools.partial(gather_kernel, members, stride, spread_out),
        out_shape=jax.ShapeDtypeStruct((members,) + own.shape, own.dtype),
        in_specs=[pl.BlockSpec(memory_space=pltpu.VMEM)],
        out_specs=pl.BlockSpec(memory_space=pltpu.VMEM),
        scratch_shapes=[
            pltpu.SemaphoreType.DMA((members - 1,)),
            pltpu.SemaphoreType.DMA((members - 1,)),
        ],
        compiler_params=pltpu.CompilerParams(
            collective_id=collective_id, has_side_effects=True
        ),
        cost_estimate=pl.CostEstimate(flops=0, bytes_accessed=20 * moved, transcendentals=0),
    )(own)


def local(queries, keys, values, segment_ids, out_weight):
    row_count = queries.shape[0]
    seq_count = lax.axis_size("seq")
    tp_count = lax.axis_size("tp")
    my_index = lax.axis_index("seq")
    per = seq_count // tp_count
    pair_width = keys.shape[1] + values.shape[1]
    id_rows = -(-row_count // pair_width)
    pad_rows = -(-id_rows // 16) * 16
    ids_low = jnp.pad(segment_ids.astype(jnp.bfloat16), (0, pad_rows * pair_width - row_count))
    packed = jnp.concatenate(
        [jnp.concatenate([keys, values], axis=1), ids_low.reshape(pad_rows, pair_width)], axis=0
    )
    weight_wide = lax.all_gather(
        out_weight,
        "seq",
        axis=1,
        tiled=True,
        axis_index_groups=[
            [t * per + r for r in range(per)] for t in range(tp_count)
        ],
    )
    gathered = direct_gather(packed, seq_count, 1, 0)
    both = gathered[:, :row_count].reshape(seq_count * row_count, pair_width)
    value_piece = both[:, keys.shape[1] :]
    all_segs = (
        gathered[:, row_count:]
        .reshape(seq_count, pad_rows * pair_width)[:, :row_count]
        .reshape(seq_count * row_count)
        .astype(jnp.int32)
    )
    totals = doc_counts_of(all_segs, SEGMENTS)
    doc_ends = jnp.cumsum(totals)
    starts = doc_ends - totals
    own_rows = my_index * row_count + jnp.arange(row_count, dtype=jnp.int32)
    positions = own_rows - first_rows(segment_ids, starts)
    query_rot = rotate_heads(queries, positions, HEAD_DIM)
    all_rows = jnp.arange(seq_count * row_count, dtype=jnp.int32)
    key_piece = rotate_heads(
        both[:, : keys.shape[1]], all_rows - first_rows(all_segs, starts), HEAD_DIM
    )
    attended = attend(
        query_rot, key_piece, value_piece, segment_ids, all_segs, own_rows[0], positions[0]
    )
    half_count = tp_count // 2 if tp_count % 2 == 0 else tp_count

    def keeper(b):
        return (b % half_count) * (tp_count // half_count) + b // half_count

    attended_all = direct_gather(attended, tp_count, per, 1, keeper).reshape(
        tp_count * row_count, attended.shape[1]
    )
    partial_value = jnp.dot(
        attended_all, weight_wide, preferred_element_type=jnp.float32
    ).astype(jnp.bfloat16)
    summed = lax.psum_scatter(partial_value, "tp", scatter_dimension=0, tiled=True)
    pairs = []
    for t in range(tp_count):
        for r in range(per):
            for b in range(tp_count):
                pairs.append(((t * per + r) * tp_count + keeper(b), (b * per + r) * tp_count + t))
    return lax.ppermute(summed, ("seq", "tp"), pairs)


def solution(mesh):
    return jax.shard_map(
        local,
        mesh=mesh,
        in_specs=(P("seq", "tp"), P("seq", "tp"), P("seq", "tp"), P("seq"), P("tp", "seq")),
        out_specs=P("seq", "tp"),
        check_vma=False,
    )
```

time: 201 us -> 190 us (0.945)
  the two profiles are of different devices: /device:TPU:4 before, /device:TPU:1 now
where the time goes in v3:
time: 190 us
  Pallas kernels  73.6 us (39%)
  waiting for transfers between devices  72 us (38%)
  between operations  15.5 us (8%)
  other arithmetic  10.5 us (6%)
  matrix products  7.76 us (4%)
  local copies, waits for them, and re-layouts  5.42 us (3%)
  starting transfers between devices  4.8 us (3%)
    pallas_call x2, Pallas kernels, direct_gather(): pl.pallas_call(functools.partial(gather_kernel, members, stride, spread_o...  68.3 us
    reduce_scatter x1, waiting for transfers between devices, local(): lax.psum_scatter(partial_value, 'tp', scatter_dimension=0, tiled=True)  45.4 us
    ppermute x1, waiting for transfers between devices, local(): return lax.ppermute(summed, ('seq', 'tp'), pairs)  25.8 us
    dot_general x1, matrix products, local(): jnp.dot(attended_all, weight_wide, preferred_element_type=jnp.float32)  7.76 us
    pallas_call x1, Pallas kernels, attend(): pl.pallas_call(functools.partial(attend_kernel, HEADS // KV_HEADS), out_s...  5.28 us
    ppermute x1, starting transfers between devices, local(): return lax.ppermute(summed, ('seq', 'tp'), pairs)  4.76 us
    another operation x4, other arithmetic  4.17 us
  transfers between devices with their start and end apart: 3, of which 2 were waited for; matrix products, arithmetic and copies ran while one was open for 8% of the time, Pallas kernels for 39%

profile of v3, /device:TPU:1, one launch (start us, length us, event | category | flops | bytes accessed | tf_op | source)
XLA Modules:
  0.0 189.5 jit_solution(8626541822740176430)
XLA Ops:
  6.5 0.7 all-gather.2.cloned.1.call-update
  7.3 0.7 convert_element_type.59
  8.0 1.5 pad_maximum_fusion.1.own_ref
  9.5 20.1 %shard_map.55 = bf16[8,208,256]{2,1,0:T(8,128)(2,1)} custom-call(bf16[208,256]{1,0:T(8,128)(2,1)} %pad_maximum_fusion.1.own_ref), custom_call_target="tpu_custom_call" | custom-call | bytes 14909440 | tf_op jit(solution)/shard_map/pallas_call | solution.py:169
  29.6 0.9 slice_bitcast_fusion.1
  30.5 0.7 reshape.251.kseg_ref
  31.7 0.6 slice.33
  33.0 0.5 slice.36
  34.8 0.8 copy.13.qseg_ref
  35.8 0.4 multiply_cosine_fusion.1
  36.2 0.4 subtract_convert_fusion
  36.6 0.2 pad_maximum_fusion
  36.9 0.8 copy.18
  37.7 1.3 pad_add_fusion.limits
  39.1 0.9 fusion.12
  39.9 3.6 %fusion.5 = (bf16[1536,1,64]{2,0,1:T(8,128)(2,1)S(1)}, bf16[1536,1,64]{2,0,1:T(8,128)(2,1)S(1)}) fusion(f32[1536,1,128]{2,0,1:T(8,128)S(1)} %get-tuple-element.12, f32[1536]{0:T(1024)S(1)} %subtract_convert_fusion.1, f32[64]{0:T(128)S(1)} %negate_power_fusion), kind=kLoop, calls=%fused_computation.8 | loop fusion | flops 884736 | bytes 1186048 | tf_op jit(solution)/shard_map/convert.4
  43.5 1.0 maximum_bitcast_fusion.key_ref
  44.5 5.3 %shard_map.56.own_ref = bf16[192,1024]{1,0:T(8,128)(2,1)} custom-call(s32[3]{0:T(128)} %pad_add_fusion.limits, bf16[192,1024]{1,0:T(8,128)(2,1)} %bitcast.31, bf16[1536,128]{1,0:T(8,128)(2,1)} %maximum_bitcast_fusion.key_ref, bf16[1536,128]{1,0:T(8,128)(2,1)} %get-tuple-element.11.value_ref, s32[192,1]{1,0:T(8,128)} %copy.13.qseg_ref, ...), custom_call_target="tpu_custom_call" | custom-call | flops 1207959552 | bytes 1572864 | tf_op jit(solution)/shard_map/pallas_call | solution.py:113
  49.8 48.2 %shard_map.57 = bf16[4,192,1024]{2,1,0:T(8,128)(2,1)} custom-call(bf16[192,1024]{1,0:T(8,128)(2,1)} %shard_map.56.own_ref), custom_call_target="tpu_custom_call" | custom-call | bytes 23592960 | tf_op jit(solution)/shard_map/pallas_call | solution.py:169
  98.0 7.8 %convolution_convert_fusion = bf16[768,2048]{1,0:T(8,128)(2,1)} fusion(bf16[768,1024]{1,0:T(8,128)(2,1)} %bitcast.30, bf16[1024,2048]{1,0:T(8,128)(2,1)} %all-gather.2.cloned.1.call-done), kind=kOutput, calls=%fused_computation | convolution fusion | flops 3222798336 | bytes 8912896 | tf_op jit(solution)/shard_map/dot_general | solution.py:237
  105.8 45.4 %reduce-scatter.2.cloned.1.call-done = bf16[192,2048]{1,0:T(8,128)(2,1)} async-done(((bf16[768,2048]{1,0:T(8,128)(2,1)}), bf16[192,2048]{1,0:T(8,128)(2,1)}) %reduce-scatter.2.cloned.1.call-update) | async-done | bytes 786448 | tf_op jit(solution)/shard_map/reduce_scatter | solution.py:240
  151.3 4.8 %collective-permute-start = (bf16[192,2048]{1,0:T(8,128)(2,1)}, bf16[192,2048]{1,0:T(8,128)(2,1)S(1)}, u32[]{:S(2)}, u32[]{:S(2)}) collective-permute-start(bf16[192,2048]{1,0:T(8,128)(2,1)} %reduce-scatter.2.cloned.1.call-done), channel_id=1, source_target_pairs={{0,0},{2,8},{1,16},{3,24},{4,4},{6,12},{5,20},{7,28},{8,1},{10,9},... | collective-permute-start | bytes 2359304 | tf_op jit(solution)/shard_map/ppermute | solution.py:246
  156.0 25.8 %collective-permute-done = bf16[192,2048]{1,0:T(8,128)(2,1)S(1)} collective-permute-done((bf16[192,2048]{1,0:T(8,128)(2,1)}, bf16[192,2048]{1,0:T(8,128)(2,1)S(1)}, u32[]{:S(2)}, u32[]{:S(2)}) %collective-permute-start) | collective-permute-done | bytes 786464 | tf_op jit(solution)/shard_map/ppermute | solution.py:246
  181.8 0.9 copy.20
  (27 shorter events, 1.0 us)
Async XLA Ops:
  6.5 25.1 %copy-start.1 = (s32[192]{0:T(256)S(1)}, s32[192]{0:T(256)}, u32[]{:S(2)}) copy-start(s32[192]{0:T(256)} %param.8) | copy-start | bytes 2308
  6.5 29.0 %copy-start = (bf16[192,1024]{1,0:T(8,128)(2,1)S(1)}, bf16[192,1024]{1,0:T(8,128)(2,1)}, u32[]{:S(2)}) copy-start(bf16[192,1024]{1,0:T(8,128)(2,1)} %param.5) | copy-start | bytes 1179652
  6.5 91.5 %all-gather.2.cloned.1.call-start = ((), (), s32[]{:S(2)}) async-start(), calls=%async_computation.1 | async-start | bytes 6291456 | tf_op jit(solution)/shard_map/all_gather | solution.py:198
  7.3 144.0 %reduce-scatter.2.cloned.1.call-start = ((), (), s32[]{:S(2)}) async-start(), calls=%async_computation.2 | async-start | bytes 3932160 | tf_op jit(solution)/shard_map/reduce_scatter | solution.py:240
  35.6 3.5 %slice-start = ((bf16[8,208,256]{2,1,0:T(8,128)(2,1)}), bf16[8,192,256]{2,1,0:T(8,128)(2,1)S(1)}, s32[]{:S(2)}) async-start(bf16[8,208,256]{2,1,0:T(8,128)(2,1)} %shard_map.55), calls=%async_computation.3 | async-start | bytes 1572864 | tf_op jit(solution)/shard_map/slice | solution.py:208
  151.3 30.5 %collective-permute-start = (bf16[192,2048]{1,0:T(8,128)(2,1)}, bf16[192,2048]{1,0:T(8,128)(2,1)S(1)}, u32[]{:S(2)}, u32[]{:S(2)}) collective-permute-start(bf16[192,2048]{1,0:T(8,128)(2,1)} %reduce-scatter.2.cloned.1.call-done), channel_id=1, source_target_pairs={{0,0},{2,8},{1,16},{3,24},{4,4},{6,12},{5,20},{7,28},{8,1},{10,9},... | collective-permute-start | bytes 2359304 | tf_op jit(solution)/shard_map/ppermute | solution.py:246
Sparse Core Ops, SparseCore 0:
  8.9 62.2 all-gather.1
  105.9 45.2 reduce-scatter.1
